TPU v7x, 32 devices: a whole 2x2x4 slice. The times are simulated.
32 devices in a mesh: node: 8 (over y, x, core), grp: 4 (over z).
Axes of the slice: x: 2, y: 2, z: 4, core: 2. Of those that a mesh axis runs over, the one named last changes fastest.
Arguments:
- tokens: bfloat16 [12288, 1792], P(('node', 'grp')), may hold values from -6 to 6
- cotangent: bfloat16 [12288, 1792], P(('node', 'grp')), may hold values from -6 to 6
- gate_weight: bfloat16 [1792, 1024], P('node'), may hold values from -0.125 to 0.125
- up_weight: bfloat16 [1792, 1024], P('node'), may hold values from -0.125 to 0.125
- down_weight_t: bfloat16 [1792, 1024], P('node'), may hold values from -0.125 to 0.125
- error_memory: bfloat16 [4, 1792, 3072], P('grp', 'node'), may hold values from -4 to 4
- q_init: float32 [3, 1024, 32], replicated, may hold values from -6 to 6
Outputs:
- token_grad: bfloat16 [12288, 1792], P(('node', 'grp'))
- new_error: bfloat16 [4, 1792, 3072], P('grp', 'node')
- p_hat: float32 [3, 1792, 32], P(None, 'node')
- q_new: float32 [3, 1024, 32], replicated
All inputs are finite; a program needn't handle non-finite values.
Results may differ from a plain program's by a relative error of at most 0.012.
Values may be sent and summed in bfloat16 or wider, within the bound.
A program may use at most 192 MiB of HBM per device.

v0:
```python
import math
import jax
import jax.numpy as jnp
from jax import lax
from jax.sharding import PartitionSpec as P


def gelu_parts(value):
    coeff = math.sqrt(2.0 / math.pi)
    inner = coeff * (value + 0.044715 * value * value * value)
    tanh_value = jnp.tanh(inner)
    activation = 0.5 * value * (1.0 + tanh_value)
    slope = 0.5 * (1.0 + tanh_value) + 0.5 * value * (1.0 - tanh_value * tanh_value) * coeff * (
        1.0 + 3.0 * 0.044715 * value * value
    )
    return (activation, slope)


def contract_rows(left_side, right_side):
    return lax.dot_general(
        left_side, right_side, (((0,), (0,)), ((), ())), preferred_element_type=jnp.float32
    )


def on_device(tokens, cotangent, gate_weight, up_weight, down_weight_t, error_memory, q_init):
    node_count = lax.axis_size("node")
    group_count = lax.axis_size("grp")
    hidden_units = gate_weight.shape[1]
    highest = lax.Precision.HIGHEST
    full_gate, full_up, full_down = (
        lax.all_gather(gate_weight, "node", axis=0, tiled=True),
        lax.all_gather(up_weight, "node", axis=0, tiled=True),
        lax.all_gather(down_weight_t, "node", axis=0, tiled=True),
    )
    gate_pre = jnp.dot(tokens, full_gate, preferred_element_type=jnp.float32)
    up_pre = jnp.dot(tokens, full_up, preferred_element_type=jnp.float32)
    activation, slope = gelu_parts(gate_pre)
    hidden = (activation * up_pre).astype(jnp.bfloat16)
    back_hidden = jnp.dot(cotangent, full_down, preferred_element_type=jnp.float32)
    grad_up = (back_hidden * activation).astype(jnp.bfloat16)
    grad_gate = (back_hidden * up_pre * slope).astype(jnp.bfloat16)
    token_grad = (
        lax.dot_general(
            grad_gate, full_gate, (((1,), (1,)), ((), ())), preferred_element_type=jnp.float32
        )
        + lax.dot_general(
            grad_up, full_up, (((1,), (1,)), ((), ())), preferred_element_type=jnp.float32
        )
    ).astype(jnp.bfloat16)
    gate_up = jnp.concatenate([grad_gate, grad_up], axis=1)
    token_cols, cot_cols = (
        lax.all_to_all(tokens, "node", split_axis=1, concat_axis=0, tiled=True),
        lax.all_to_all(cotangent, "node", split_axis=1, concat_axis=0, tiled=True),
    )
    piece_gu = lax.all_gather(gate_up, "node", axis=0, tiled=True)
    piece_hidden = lax.all_gather(hidden, "node", axis=0, tiled=True)
    summed = jnp.concatenate(
        [contract_rows(token_cols, piece_gu), contract_rows(cot_cols, piece_hidden)], axis=1
    )
    grad_scale = 1.0 / math.sqrt(tokens.shape[0] * node_count)
    merged = summed * grad_scale + error_memory[0].astype(jnp.float32)
    blocks = [merged[:, m * hidden_units : (m + 1) * hidden_units] for m in range(3)]
    row_terms = jnp.stack([jnp.dot(blocks[m], q_init[m], precision=highest) for m in range(3)])
    power_rows = lax.psum(row_terms.astype(jnp.bfloat16), "grp").astype(jnp.float32) / group_count
    local_gram = jnp.einsum("mdr,mds->mrs", power_rows, power_rows, precision=highest)
    gram_matrix = lax.psum(local_gram, "node")
    hats = []
    for m in range(3):
        factor = jnp.linalg.cholesky(gram_matrix[m])
        hats.append(jax.scipy.linalg.solve_triangular(factor, power_rows[m].T, lower=True).T)
    col_terms = jnp.stack([jnp.dot(blocks[m].T, hats[m], precision=highest) for m in range(3)])
    q_new = lax.psum(col_terms, ("node", "grp")) / group_count
    errors = [blocks[m] - jnp.dot(hats[m], q_new[m].T, precision=highest) for m in range(3)]
    new_error = jnp.concatenate(errors, axis=1).astype(jnp.bfloat16)[None]
    return (token_grad, new_error, jnp.stack(hats), q_new)


def solution(mesh):
    return jax.shard_map(
        on_device,
        mesh=mesh,
        in_specs=(
            P(("node", "grp"), None),
            P(("node", "grp"), None),
            P("node", None),
            P("node", None),
            P("node", None),
            P("grp", "node", None),
            P(),
        ),
        out_specs=(P(("node", "grp"), None), P("grp", "node", None), P(None, "node", None), P()),
        check_vma=False,
    )
```

profile of v0, /device:TPU:0, one launch (start us, length us, event | category | flops | bytes accessed | tf_op | source)
XLA Modules:
  0.0 512.1 jit_solution(15546751805123783097)
XLA Ops:
  9.4 37.6 %all-gather.6.cloned.1.call-done = bf16[1792,1024]{1,0:T(8,128)(2,1)} async-done(((bf16[224,1024]{1,0:T(8,128)(2,1)}), bf16[1792,1024]{1,0:T(8,128)(2,1)}) %all-gather.6.cloned.1.call-update) | async-done | bytes 3670032 | tf_op jit(solution)/shard_map/all_gather | solution.py:33
  47.0 5.2 %fusion.44 = f32[384,1024]{1,0:T(8,128)} fusion(bf16[384,1792]{1,0:T(8,128)(2,1)} %param.11, bf16[1792,1024]{1,0:T(8,128)(2,1)} %all-gather.6.cloned.1.call-done), kind=kOutput, calls=%fused_computation.92 | convolution fusion | flops 1409286144 | bytes 6619136 | tf_op jit(solution)/shard_map/dot_general | solution.py:39
  52.2 31.1 %all-gather.10.cloned.1.call-done = bf16[1792,1024]{1,0:T(8,128)(2,1)} async-done(((bf16[224,1024]{1,0:T(8,128)(2,1)}), bf16[1792,1024]{1,0:T(8,128)(2,1)}) %all-gather.10.cloned.1.call-update) | async-done | bytes 3670032 | tf_op jit(solution)/shard_map/all_gather | solution.py:31
  83.3 4.8 fusion.45
  88.1 31.5 %all-gather.8.cloned.1.call-done = bf16[1792,1024]{1,0:T(8,128)(2,1)} async-done(((bf16[224,1024]{1,0:T(8,128)(2,1)}), bf16[1792,1024]{1,0:T(8,128)(2,1)}) %all-gather.8.cloned.1.call-update) | async-done | bytes 3670032 | tf_op jit(solution)/shard_map/all_gather | solution.py:32
  119.6 6.4 %multiply_convert_fusion = (bf16[384,1024]{1,0:T(8,128)(2,1)}, bf16[384,1024]{1,0:T(8,128)(2,1)S(1)}, bf16[384,1024]{1,0:T(8,128)(2,1)S(1)}) fusion(f32[384,1024]{1,0:T(8,128)} %fusion.45, f32[384,1024]{1,0:T(8,128)} %fusion.44, bf16[384,1792]{1,0:T(8,128)(2,1)S(1)} %copy-done.2, bf16[1792,1024]{1,0:T(8,128)(2,1)} %all-gather.8.cloned.1.call-done), kind=kOutput, calls=%fused_computation.15 | convolution fusion | flops 1419116544 | bytes 10551296 | tf_op jit(solution)/shard_map/dot_general | solution.py:36
  131.1 3.6 all-to-all-start.1
  136.3 24.3 %all-to-all-done.1 = bf16[384,8,224]{0,2,1:T(8,128)(2,1)S(1)} async-done(((bf16[384,8,224]{0,2,1:T(8,128)(2,1)}), bf16[384,8,224]{0,2,1:T(8,128)(2,1)S(1)}, u32[]{:S(2)}, u32[]{:S(2)}) %all-to-all-start.1) | async-done | bytes 1376288 | tf_op jit(solution)/shard_map/all_to_all | solution.py:53
  160.5 3.6 all-to-all-start
  165.7 31.9 %all-to-all-done = bf16[384,8,224]{0,2,1:T(8,128)(2,1)S(1)} async-done(((bf16[384,8,224]{0,2,1:T(8,128)(2,1)}), bf16[384,8,224]{0,2,1:T(8,128)(2,1)S(1)}, u32[]{:S(2)}, u32[]{:S(2)}) %all-to-all-start) | async-done | bytes 1376288 | tf_op jit(solution)/shard_map/all_to_all | solution.py:52
  198.9 5.4 %fusion.46 = f32[384,1792]{1,0:T(8,128)} fusion(bf16[384,1024]{1,0:T(8,128)(2,1)S(1)} %copy-done.8, bf16[1792,1024]{1,0:T(8,128)(2,1)} %all-gather.10.cloned.1.call-done), kind=kOutput, calls=%fused_computation.94 | convolution fusion | flops 1409286144 | bytes 7208960 | tf_op jit(solution)/shard_map/dot_general | solution.py:43
  204.3 5.4 %convolution_bitcast_fusion.1 = f32[224,1024]{1,0:T(8,128)} fusion(bf16[3072,224]{0,1:T(8,128)(2,1)S(1)} %bitcast.133, bf16[3072,1024]{1,0:T(8,128)(2,1)} %all-gather.14.cloned.1.call-done), kind=kOutput, calls=%fused_computation.19 | convolution fusion | flops 1409286144 | bytes 8585216 | tf_op jit(solution)/shard_map/dot_general | solution.py:20
  209.7 64.7 %all-gather.12.cloned.1.call-done = bf16[3072,2048]{1,0:T(8,128)(2,1)} async-done(((bf16[384,2048]{1,0:T(8,128)(2,1)}), bf16[3072,2048]{1,0:T(8,128)(2,1)}) %all-gather.12.cloned.1.call-update) | async-done | bytes 12582928 | tf_op jit(solution)/shard_map/all_gather | solution.py:55
  274.4 6.4 %convolution_bitcast_fusion = f32[224,2048]{1,0:T(8,128)S(1)} fusion(bf16[3072,224]{0,1:T(8,128)(2,1)S(1)} %bitcast.134, bf16[3072,2048]{1,0:T(8,128)(2,1)} %all-gather.12.cloned.1.call-done), kind=kOutput, calls=%fused_computation.4 | convolution fusion | flops 2818572288 | bytes 15794176 | tf_op jit(solution)/shard_map/dot_general | solution.py:20
  285.2 20.5 %psum.21 = bf16[3,224,32]{1,2,0:T(8,128)(2,1)} all-reduce(bf16[3,224,32]{1,2,0:T(8,128)(2,1)} %pad_maximum_fusion.4), channel_id=1, replica_groups=mesh['node'=8,'grp'=4] {'grp'}, use_global_device_ids=true, to_apply=%region_0.0 | all-reduce | flops 21504 | bytes 86016 | tf_op jit(solution)/shard_map/psum | solution.py:64
  308.8 24.0 %psum.22 = f32[3,32,32]{1,2,0:T(8,128)} all-reduce(f32[3,32,32]{1,2,0:T(8,128)} %fusion.33), channel_id=1, replica_groups=mesh['node'=8,'grp'=4] {'node'}, use_global_device_ids=true, to_apply=%region_1.0 | all-reduce | flops 3072 | bytes 24576 | tf_op jit(solution)/shard_map/psum | solution.py:66
  339.2 3.6 cholesky.59
  344.8 3.8 custom-call.7
  348.5 3.6 cholesky.70
  354.1 3.2 custom-call.8
  360.5 3.6 cholesky.81
  366.0 3.2 custom-call.9
  373.8 5.7 %fusion = bf16[384,1792]{1,0:T(8,128)(2,1)} fusion(f32[384,1792]{1,0:T(8,128)} %fusion.46, bf16[384,1024]{1,0:T(8,128)(2,1)S(1)} %get-tuple-element.8, bf16[1792,1024]{1,0:T(8,128)(2,1)} %all-gather.8.cloned.1.call-done), kind=kOutput, calls=%fused_computation.1 | convolution fusion | flops 1410662400 | bytes 8585216 | tf_op jit(solution)/shard_map/dot_general | solution.py:46
  380.2 119.2 %all-reduce.2.cloned.1.call-done = f32[3,1024,32]{1,2,0:T(8,128)} async-done(((f32[3,1024,32]{1,2,0:T(8,128)}), f32[3,1024,32]{1,2,0:T(8,128)}) %all-reduce.2.cloned.1.call-update) | async-done | bytes 393232 | tf_op jit(solution)/shard_map/psum | solution.py:72
  (86 shorter events, 45.6 us)
Async XLA Ops:
  7.2 39.8 %all-gather.6.cloned.1.call-start = ((), (), s32[]{:S(2)}) async-start(), calls=%async_computation.2 | async-start | bytes 4128768 | tf_op jit(solution)/shard_map/all_gather | solution.py:33
  7.9 75.4 %all-gather.10.cloned.1.call-start = ((), (), s32[]{:S(2)}) async-start(), calls=%async_computation.4 | async-start | bytes 4128768 | tf_op jit(solution)/shard_map/all_gather | solution.py:31
  8.6 111.0 %all-gather.8.cloned.1.call-start = ((), (), s32[]{:S(2)}) async-start(), calls=%async_computation.3 | async-start | bytes 4128768 | tf_op jit(solution)/shard_map/all_gather | solution.py:32
  9.4 73.9 %copy-start.2 = (bf16[384,1792]{1,0:T(8,128)(2,1)S(1)}, bf16[384,1792]{1,0:T(8,128)(2,1)}, u32[]{:S(2)}) copy-start(bf16[384,1792]{1,0:T(8,128)(2,1)} %param.10) | copy-start | bytes 4128772
  9.4 194.9 %all-gather.14.cloned.1.call-start = ((), (), s32[]{:S(2)}) async-start(), calls=%async_computation.6 | async-start | bytes 7077888 | tf_op jit(solution)/shard_map/all_gather | solution.py:56
  126.0 148.4 %all-gather.12.cloned.1.call-start = ((), (), s32[]{:S(2)}) async-start(), calls=%async_computation.5 | async-start | bytes 14155776 | tf_op jit(solution)/shard_map/all_gather | solution.py:55
  128.2 1.3 copy-start.1
  131.1 29.4 %all-to-all-start.1 = ((bf16[384,8,224]{0,2,1:T(8,128)(2,1)}), bf16[384,8,224]{0,2,1:T(8,128)(2,1)S(1)}, u32[]{:S(2)}, u32[]{:S(2)}) async-start(bf16[384,8,224]{0,2,1:T(8,128)(2,1)} %bitcast.3), calls=%async_computation.1 | async-start | bytes 2752512 | tf_op jit(solution)/shard_map/all_to_all | solution.py:53
  160.5 37.1 %all-to-all-start = ((bf16[384,8,224]{0,2,1:T(8,128)(2,1)}), bf16[384,8,224]{0,2,1:T(8,128)(2,1)S(1)}, u32[]{:S(2)}, u32[]{:S(2)}) async-start(bf16[384,8,224]{0,2,1:T(8,128)(2,1)} %bitcast), calls=%async_computation | async-start | bytes 2752512 | tf_op jit(solution)/shard_map/all_to_all | solution.py:52
  164.1 335.3 %all-reduce.2.cloned.1.call-start = ((), (), s32[]{:S(2)}) async-start(), calls=%async_computation.7 | async-start | bytes 786432 | tf_op jit(solution)/shard_map/psum | solution.py:72
  197.6 1.3 copy-start.8
  198.9 5.4 %copy-start.4 = (bf16[8,28,8,384]{3,2,0,1:T(8,128)(2,1)S(1)}, bf16[8,28,8,384]{3,2,0,1:T(8,128)(2,1)}, u32[]{:S(2)}) copy-start(bf16[8,28,8,384]{3,2,0,1:T(8,128)(2,1)} %copy.25) | copy-start | bytes 4128772
  204.3 70.1 %copy-start.5 = (bf16[8,28,8,384]{3,2,0,1:T(8,128)(2,1)S(1)}, bf16[8,28,8,384]{3,2,0,1:T(8,128)(2,1)}, u32[]{:S(2)}) copy-start(bf16[8,28,8,384]{3,2,0,1:T(8,128)(2,1)} %copy.24) | copy-start | bytes 4128772
  274.4 6.4 %copy-start.3 = (bf16[1,224,3072]{2,1,0:T(8,128)(2,1)S(1)}, bf16[1,224,3072]{2,1,0:T(8,128)(2,1)}, u32[]{:S(2)}) copy-start(bf16[1,224,3072]{2,1,0:T(8,128)(2,1)} %param.15) | copy-start | bytes 4128772
  274.4 6.4 %copy-start.6 = (f32[224,1024]{1,0:T(8,128)S(1)}, f32[224,1024]{1,0:T(8,128)}, u32[]{:S(2)}) copy-start(f32[224,1024]{1,0:T(8,128)} %convolution_bitcast_fusion.1) | copy-start | bytes 2752516
  280.8 1.0 copy-start.16
  369.2 3.1 copy-start.9
  370.2 2.8 copy-start.14
  373.8 5.7 %copy-start.10 = (f32[32,224]{1,0:T(8,128)S(1)}, f32[32,224]{1,0:T(8,128)}, u32[]{:S(2)}) copy-start(f32[32,224]{1,0:T(8,128)} %fusion.32) | copy-start | bytes 86020
  373.8 5.7 %copy-start.12 = (f32[32,224]{1,0:T(8,128)S(1)}, f32[32,224]{1,0:T(8,128)}, u32[]{:S(2)}) copy-start(f32[32,224]{1,0:T(8,128)} %fusion.31) | copy-start | bytes 86020
  373.8 5.7 %copy-start.15 = (f32[32,224]{1,0:T(8,128)S(1)}, f32[32,224]{1,0:T(8,128)}, u32[]{:S(2)}) copy-start(f32[32,224]{1,0:T(8,128)} %copy-done.14) | copy-start | bytes 86020
  379.5 122.7 %copy-start.13 = (f32[32,224]{1,0:T(8,128)S(1)}, f32[32,224]{1,0:T(8,128)}, u32[]{:S(2)}) copy-start(f32[32,224]{1,0:T(8,128)} %fusion.31) | copy-start | bytes 86020
  500.4 3.7 copy-start
  500.4 2.7 copy-start.11
  (1 other events, 0.9 us)
Sparse Core Ops, SparseCore 0:
  9.9 37.0 all-gather.5
  48.9 34.3 all-gather.9
  85.2 34.3 all-gather.7
  126.1 74.4 all-gather.13
  202.4 71.9 all-gather.11
  373.9 125.4 all-reduce.1
where the time goes:
time: 514 us; the launch traced here: 512 us
  waiting for transfers between devices  342 us (67%)
  matrix products  54.2 us (11%)
  blocking collectives  44.5 us (9%)
  other arithmetic  35.7 us (7%)
  between operations  14.4 us (3%)
  local copies, waits for them, and re-layouts  13.4 us (3%)
  starting transfers between devices  7.6 us (1%)
    psum x1, waiting for transfers between devices, on_device(): q_new = lax.psum(col_terms, ('node', 'grp')) / group_count  119 us
    all_gather x1, waiting for transfers between devices, on_device(): piece_gu = lax.all_gather(gate_up, 'node', axis=0, tiled=True)  64.7 us
    all_gather x1, waiting for transfers between devices, on_device(): lax.all_gather(down_weight_t, 'node', axis=0, tiled=True)  37.6 us
    all_to_all x1, waiting for transfers between devices, on_device(): lax.all_to_all(tokens, 'node', split_axis=1, concat_axis=0, tiled=True)  31.9 us
    all_gather x1, waiting for transfers between devices, on_device(): lax.all_gather(up_weight, 'node', axis=0, tiled=True)  31.5 us
    all_gather x1, waiting for transfers between devices, on_device(): lax.all_gather(gate_weight, 'node', axis=0, tiled=True)  31.1 us
    all_to_all x1, waiting for transfers between devices, on_device(): lax.all_to_all(cotangent, 'node', split_axis=1, concat_axis=0, tiled=True)  24.3 us
    psum x1, blocking collectives, on_device(): gram_matrix = lax.psum(local_gram, 'node')  24 us
  transfers between devices with their start and end apart: 8, of which 7 were waited for; matrix products, arithmetic and copies ran while one was open for 7% of the time, Pallas kernels for 0%

commit v1 on v0

--- a/solution.py
+++ b/solution.py
@@ -52,7 +52,12 @@
         lax.all_to_all(tokens, "node", split_axis=1, concat_axis=0, tiled=True),
         lax.all_to_all(cotangent, "node", split_axis=1, concat_axis=0, tiled=True),
     )
-    piece_gu = lax.all_gather(gate_up, "node", axis=0, tiled=True)
+    ring = [gate_up]
+    for hop in range(7):
+        ring.append(lax.ppermute(ring[-1], "node", [(dev, (dev + 1) % 8) for dev in range(8)]))
+    piece_gu = jnp.roll(
+        jnp.concatenate(ring[::-1], axis=0), (lax.axis_index("node") + 1) * ring[0].shape[0], axis=0
+    )
     piece_hidden = lax.all_gather(hidden, "node", axis=0, tiled=True)
     summed = jnp.concatenate(
         [contract_rows(token_cols, piece_gu), contract_rows(cot_cols, piece_hidden)], axis=1

time: 514 us -> 594 us (1.16)
  waiting for transfers between devices: 342 us -> 383 us
  local copies, waits for them, and re-layouts: 13.4 us -> 49.9 us
    ppermute x0 -> x7, waiting for transfers between devices: none -> 152 us  [on_device(): lax.ppermute(ring[-1], 'node', [(dev, (dev + 1) % 8) for dev in range(8)])]
    all_gather x1 -> x0, waiting for transfers between devices: 64.7 us -> none  [on_device(): piece_gu = lax.all_gather(gate_up, 'node', axis=0, tiled=True)]
    unnamed x36 -> x50, local copies, waits for them, and re-layouts: 5.8 us -> 39.6 us
    all_to_all x1, waiting for transfers between devices: 31.9 us -> 4.75 us  [on_device(): lax.all_to_all(tokens, 'node', split_axis=1, concat_axis=0, tiled=True)]
    all_to_all x1, waiting for transfers between devices: 24.3 us -> 4.91 us  [on_device(): lax.all_to_all(cotangent, 'node', split_axis=1, concat_axis=0, tiled=True)]
    all_gather x1, waiting for transfers between devices: 37.6 us -> 31.1 us  [on_device(): lax.all_gather(down_weight_t, 'node', axis=0, tiled=True)]
    all_gather x1, waiting for transfers between devices: 31.1 us -> 37.6 us  [on_device(): lax.all_gather(gate_weight, 'node', axis=0, tiled=True)]
  transfers between devices with their start and end apart: 8 -> 14, of which waited for: 7 -> 13; matrix products, arithmetic and copies ran while one was open for 7% -> 6% of each run, Pallas kernels for 0% -> 0%
where the time goes in v1:
time: 594 us; the launch traced here: 592 us
  waiting for transfers between devices  383 us (64%)
  matrix products  53.5 us (9%)
  local copies, waits for them, and re-layouts  49.9 us (8%)
  blocking collectives  44.7 us (8%)
  other arithmetic  37.7 us (6%)
  between operations  14 us (2%)
  starting transfers between devices  9.08 us (2%)
    ppermute x7, waiting for transfers between devices, on_device(): lax.ppermute(ring[-1], 'node', [(dev, (dev + 1) % 8) for dev in range(8)])  152 us
    psum x1, waiting for transfers between devices, on_device(): q_new = lax.psum(col_terms, ('node', 'grp')) / group_count  119 us
    unnamed x50, local copies, waits for them, and re-layouts  39.6 us
    all_gather x1, waiting for transfers between devices, on_device(): lax.all_gather(gate_weight, 'node', axis=0, tiled=True)  37.6 us
    all_gather x1, waiting for transfers between devices, on_device(): lax.all_gather(up_weight, 'node', axis=0, tiled=True)  31.5 us
    all_gather x1, waiting for transfers between devices, on_device(): lax.all_gather(down_weight_t, 'node', axis=0, tiled=True)  31.1 us
    psum x1, blocking collectives, on_device(): gram_matrix = lax.psum(local_gram, 'node')  24 us
    psum x1, blocking collectives, on_device(): lax.psum(row_terms.astype(jnp.bfloat16), 'grp').astype(jnp.float32)  20.6 us
  transfers between devices with their start and end apart: 14, of which 13 were waited for; matrix products, arithmetic and copies ran while one was open for 6% of the time, Pallas kernels for 0%

profile of v1, /device:TPU:0, one launch (start us, length us, event | category | flops | bytes accessed | tf_op | source)
XLA Modules:
  0.0 592.0 jit_solution(326990745394928293)
XLA Ops:
  9.4 37.6 %all-gather.9.cloned.1.call-done = bf16[1792,1024]{1,0:T(8,128)(2,1)} async-done(((bf16[224,1024]{1,0:T(8,128)(2,1)}), bf16[1792,1024]{1,0:T(8,128)(2,1)}) %all-gather.9.cloned.1.call-update) | async-done | bytes 3670032 | tf_op jit(solution)/shard_map/all_gather | solution.py:31
  47.0 5.2 fusion.51
  52.2 31.1 %all-gather.5.cloned.1.call-done = bf16[1792,1024]{1,0:T(8,128)(2,1)} async-done(((bf16[224,1024]{1,0:T(8,128)(2,1)}), bf16[1792,1024]{1,0:T(8,128)(2,1)}) %all-gather.5.cloned.1.call-update) | async-done | bytes 3670032 | tf_op jit(solution)/shard_map/all_gather | solution.py:33
  83.3 4.8 fusion.50
  88.1 31.5 %all-gather.7.cloned.1.call-done = bf16[1792,1024]{1,0:T(8,128)(2,1)} async-done(((bf16[224,1024]{1,0:T(8,128)(2,1)}), bf16[1792,1024]{1,0:T(8,128)(2,1)}) %all-gather.7.cloned.1.call-update) | async-done | bytes 3670032 | tf_op jit(solution)/shard_map/all_gather | solution.py:32
  119.6 6.4 %multiply_convert_fusion = (bf16[384,1024]{1,0:T(8,128)(2,1)}, bf16[384,1024]{1,0:T(8,128)(2,1)S(1)}, bf16[384,1024]{1,0:T(8,128)(2,1)S(1)}) fusion(f32[384,1024]{1,0:T(8,128)} %fusion.51, f32[384,1024]{1,0:T(8,128)} %fusion.50, bf16[384,1792]{1,0:T(8,128)(2,1)S(1)} %copy-done.6, bf16[1792,1024]{1,0:T(8,128)(2,1)} %all-gather.7.cloned.1.call-done), kind=kOutput, calls=%fused_computation.17 | convolution fusion | flops 1419116544 | bytes 10551296 | tf_op jit(solution)/shard_map/dot_general | solution.py:36
  126.4 28.9 %collective-permute-done = bf16[384,2048]{1,0:T(8,128)(2,1)S(1)} collective-permute-done((bf16[384,2048]{1,0:T(8,128)(2,1)S(1)}, bf16[384,2048]{1,0:T(8,128)(2,1)S(1)}, u32[]{:S(2)}, u32[]{:S(2)}) %collective-permute-start) | collective-permute-done | bytes 1572896 | tf_op jit(solution)/shard_map/ppermute | solution.py:57
  155.3 36.1 %collective-permute-done.1 = bf16[384,2048]{1,0:T(8,128)(2,1)S(1)} collective-permute-done((bf16[384,2048]{1,0:T(8,128)(2,1)S(1)}, bf16[384,2048]{1,0:T(8,128)(2,1)S(1)}, u32[]{:S(2)}, u32[]{:S(2)}) %collective-permute-start.1) | collective-permute-done | bytes 1572896 | tf_op jit(solution)/shard_map/ppermute | solution.py:57
  192.6 20.7 %collective-permute-done.2 = bf16[384,2048]{1,0:T(8,128)(2,1)S(1)} collective-permute-done((bf16[384,2048]{1,0:T(8,128)(2,1)S(1)}, bf16[384,2048]{1,0:T(8,128)(2,1)S(1)}, u32[]{:S(2)}, u32[]{:S(2)}) %collective-permute-start.2) | collective-permute-done | bytes 1572896 | tf_op jit(solution)/shard_map/ppermute | solution.py:57
  214.5 20.8 %collective-permute-done.3 = bf16[384,2048]{1,0:T(8,128)(2,1)} collective-permute-done((bf16[384,2048]{1,0:T(8,128)(2,1)S(1)}, bf16[384,2048]{1,0:T(8,128)(2,1)}, u32[]{:S(2)}, u32[]{:S(2)}) %collective-permute-start.3) | collective-permute-done | bytes 1572896 | tf_op jit(solution)/shard_map/ppermute | solution.py:57
  237.8 4.3 all-to-all-start.1
  242.1 21.6 %collective-permute-done.4 = bf16[384,2048]{1,0:T(8,128)(2,1)} collective-permute-done((bf16[384,2048]{1,0:T(8,128)(2,1)}, bf16[384,2048]{1,0:T(8,128)(2,1)}, u32[]{:S(2)}, u32[]{:S(2)}) %collective-permute-start.4) | collective-permute-done | bytes 1572896 | tf_op jit(solution)/shard_map/ppermute | solution.py:57
  266.3 4.9 all-to-all-done.1
  271.2 4.3 all-to-all-start
  275.5 19.9 %collective-permute-done.5 = bf16[384,2048]{1,0:T(8,128)(2,1)} collective-permute-done((bf16[384,2048]{1,0:T(8,128)(2,1)}, bf16[384,2048]{1,0:T(8,128)(2,1)}, u32[]{:S(2)}, u32[]{:S(2)}) %collective-permute-start.5) | collective-permute-done | bytes 1572896 | tf_op jit(solution)/shard_map/ppermute | solution.py:57
  298.1 4.8 all-to-all-done
  305.5 5.2 fusion.52
  310.7 4.8 convolution_bitcast_fusion
  315.5 4.2 collective-permute-done.6
  352.2 6.4 %fusion.4 = f32[224,2048]{1,0:T(8,128)S(1)} fusion(bf16[3072,224]{0,1:T(8,128)(2,1)S(1)} %bitcast.132, bf16[6144,2048]{1,0:T(8,128)(2,1)} %constant_dynamic-update-slice_fusion, s32[]{:T(128)S(6)} %select_n.17), kind=kOutput, calls=%fused_computation.6 | convolution fusion | flops 2818572288 | bytes 15794180 | tf_op jit(solution)/shard_map/dot_general | solution.py:20
  363.0 20.6 %psum.21 = bf16[3,224,32]{1,2,0:T(8,128)(2,1)} all-reduce(bf16[3,224,32]{1,2,0:T(8,128)(2,1)} %pad_maximum_fusion.4), channel_id=1, replica_groups=mesh['node'=8,'grp'=4] {'grp'}, use_global_device_ids=true, to_apply=%region_0.1 | all-reduce | flops 21504 | bytes 86016 | tf_op jit(solution)/shard_map/psum | solution.py:69
  386.7 24.0 %psum.22 = f32[3,32,32]{1,2,0:T(8,128)} all-reduce(f32[3,32,32]{1,2,0:T(8,128)} %fusion.38), channel_id=1, replica_groups=mesh['node'=8,'grp'=4] {'node'}, use_global_device_ids=true, to_apply=%region_1.2 | all-reduce | flops 3072 | bytes 24576 | tf_op jit(solution)/shard_map/psum | solution.py:71
  453.6 5.7 fusion.2
  459.9 119.0 %all-reduce.2.cloned.1.call-done = f32[3,1024,32]{1,2,0:T(8,128)} async-done(((f32[3,1024,32]{1,2,0:T(8,128)}), f32[3,1024,32]{1,2,0:T(8,128)}) %all-reduce.2.cloned.1.call-update) | async-done | bytes 393232 | tf_op jit(solution)/shard_map/psum | solution.py:77
  (113 shorter events, 105.2 us)
Async XLA Ops:
  7.2 39.8 %all-gather.9.cloned.1.call-start = ((), (), s32[]{:S(2)}) async-start(), calls=%async_computation.4 | async-start | bytes 4128768 | tf_op jit(solution)/shard_map/all_gather | solution.py:31
  7.9 75.4 %all-gather.5.cloned.1.call-start = ((), (), s32[]{:S(2)}) async-start(), calls=%async_computation.2 | async-start | bytes 4128768 | tf_op jit(solution)/shard_map/all_gather | solution.py:33
  8.6 111.0 %all-gather.7.cloned.1.call-start = ((), (), s32[]{:S(2)}) async-start(), calls=%async_computation.3 | async-start | bytes 4128768 | tf_op jit(solution)/shard_map/all_gather | solution.py:32
  9.4 73.9 %copy-start.5 = (bf16[384,1792]{1,0:T(8,128)(2,1)S(1)}, bf16[384,1792]{1,0:T(8,128)(2,1)}, u32[]{:S(2)}) copy-start(bf16[384,1792]{1,0:T(8,128)(2,1)} %param.11) | copy-start | bytes 4128772
  9.4 301.3 %all-gather.11.cloned.1.call-start = ((), (), s32[]{:S(2)}) async-start(), calls=%async_computation.5 | async-start | bytes 7077888 | tf_op jit(solution)/shard_map/all_gather | solution.py:61
  52.2 67.4 %copy-start.6 = (bf16[384,1792]{1,0:T(8,128)(2,1)S(1)}, bf16[384,1792]{1,0:T(8,128)(2,1)}, u32[]{:S(2)}) copy-start(bf16[384,1792]{1,0:T(8,128)(2,1)} %param.10) | copy-start | bytes 4128772
  126.1 29.2 %collective-permute-start = (bf16[384,2048]{1,0:T(8,128)(2,1)S(1)}, bf16[384,2048]{1,0:T(8,128)(2,1)S(1)}, u32[]{:S(2)}, u32[]{:S(2)}) collective-permute-start(bf16[384,2048]{1,0:T(8,128)(2,1)S(1)} %pad_maximum_fusion), channel_id=1, source_target_pairs={{0,4},{4,8},{8,12},{12,16},{16,20},{20,24},{24,28},{28,0},{1,5},{5... | collective-permute-start | bytes 4718600 | tf_op jit(solution)/shard_map/ppermute | solution.py:57
  155.3 36.1 %collective-permute-start.1 = (bf16[384,2048]{1,0:T(8,128)(2,1)S(1)}, bf16[384,2048]{1,0:T(8,128)(2,1)S(1)}, u32[]{:S(2)}, u32[]{:S(2)}) collective-permute-start(bf16[384,2048]{1,0:T(8,128)(2,1)S(1)} %collective-permute-done), channel_id=1, source_target_pairs={{0,4},{4,8},{8,12},{12,16},{16,20},{20,24},{24,28},{28,0},{1,5},{5... | collective-permute-start | bytes 4718600 | tf_op jit(solution)/shard_map/ppermute | solution.py:57
  192.6 20.7 %collective-permute-start.2 = (bf16[384,2048]{1,0:T(8,128)(2,1)S(1)}, bf16[384,2048]{1,0:T(8,128)(2,1)S(1)}, u32[]{:S(2)}, u32[]{:S(2)}) collective-permute-start(bf16[384,2048]{1,0:T(8,128)(2,1)S(1)} %collective-permute-done.1), channel_id=1, source_target_pairs={{0,4},{4,8},{8,12},{12,16},{16,20},{20,24},{24,28},{28,0},{1,5},{5... | collective-permute-start | bytes 4718600 | tf_op jit(solution)/shard_map/ppermute | solution.py:57
  214.5 20.8 %collective-permute-start.3 = (bf16[384,2048]{1,0:T(8,128)(2,1)S(1)}, bf16[384,2048]{1,0:T(8,128)(2,1)}, u32[]{:S(2)}, u32[]{:S(2)}) collective-permute-start(bf16[384,2048]{1,0:T(8,128)(2,1)S(1)} %collective-permute-done.2), channel_id=1, source_target_pairs={{0,4},{4,8},{8,12},{12,16},{16,20},{20,24},{24,28},{28,0},{1,5},{5... | collective-permute-start | bytes 4718600 | tf_op jit(solution)/shard_map/ppermute | solution.py:57
  235.3 28.4 %collective-permute-start.4 = (bf16[384,2048]{1,0:T(8,128)(2,1)}, bf16[384,2048]{1,0:T(8,128)(2,1)}, u32[]{:S(2)}, u32[]{:S(2)}) collective-permute-start(bf16[384,2048]{1,0:T(8,128)(2,1)} %collective-permute-done.3), channel_id=1, source_target_pairs={{0,4},{4,8},{8,12},{12,16},{16,20},{20,24},{24,28},{28,0},{1,5},{5... | collective-permute-start | bytes 4718600 | tf_op jit(solution)/shard_map/ppermute | solution.py:57
  237.8 33.3 %all-to-all-start.1 = ((bf16[384,8,224]{0,2,1:T(8,128)(2,1)}), bf16[384,8,224]{0,2,1:T(8,128)(2,1)}, u32[]{:S(2)}, u32[]{:S(2)}) async-start(bf16[384,8,224]{0,2,1:T(8,128)(2,1)} %bitcast.131), calls=%async_computation.1 | async-start | bytes 2752512 | tf_op jit(solution)/shard_map/all_to_all | solution.py:53
  263.8 31.6 %collective-permute-start.5 = (bf16[384,2048]{1,0:T(8,128)(2,1)}, bf16[384,2048]{1,0:T(8,128)(2,1)}, u32[]{:S(2)}, u32[]{:S(2)}) collective-permute-start(bf16[384,2048]{1,0:T(8,128)(2,1)} %collective-permute-done.4), channel_id=1, source_target_pairs={{0,4},{4,8},{8,12},{12,16},{16,20},{20,24},{24,28},{28,0},{1,5},{5... | collective-permute-start | bytes 4718600 | tf_op jit(solution)/shard_map/ppermute | solution.py:57
  271.2 31.6 %all-to-all-start = ((bf16[384,8,224]{0,2,1:T(8,128)(2,1)}), bf16[384,8,224]{0,2,1:T(8,128)(2,1)}, u32[]{:S(2)}, u32[]{:S(2)}) async-start(bf16[384,8,224]{0,2,1:T(8,128)(2,1)} %bitcast.130), calls=%async_computation | async-start | bytes 2752512 | tf_op jit(solution)/shard_map/all_to_all | solution.py:52
  275.5 303.5 %all-reduce.2.cloned.1.call-start = ((), (), s32[]{:S(2)}) async-start(), calls=%async_computation.6 | async-start | bytes 786432 | tf_op jit(solution)/shard_map/psum | solution.py:77
  295.4 24.3 %collective-permute-start.6 = (bf16[384,2048]{1,0:T(8,128)(2,1)}, bf16[384,2048]{1,0:T(8,128)(2,1)}, u32[]{:S(2)}, u32[]{:S(2)}) collective-permute-start(bf16[384,2048]{1,0:T(8,128)(2,1)} %collective-permute-done.5), channel_id=1, source_target_pairs={{0,4},{4,8},{8,12},{12,16},{16,20},{20,24},{24,28},{28,0},{1,5},{5... | collective-permute-start | bytes 4718600 | tf_op jit(solution)/shard_map/ppermute | solution.py:57
  325.1 5.8 copy-start.3
  328.0 4.2 copy-start.1
  352.2 6.4 %copy-start.7 = (bf16[1,224,3072]{2,1,0:T(8,128)(2,1)S(1)}, bf16[1,224,3072]{2,1,0:T(8,128)(2,1)}, u32[]{:S(2)}) copy-start(bf16[1,224,3072]{2,1,0:T(8,128)(2,1)} %param.15) | copy-start | bytes 4128772
  453.6 5.7 copy-start.10
  453.6 5.7 copy-start.12
  453.6 5.7 copy-start.14
  459.3 124.1 %copy-start.15 = (f32[32,224]{1,0:T(8,128)S(1)}, f32[32,224]{1,0:T(8,128)}, u32[]{:S(2)}) copy-start(f32[32,224]{1,0:T(8,128)} %copy-done.13) | copy-start | bytes 86020
  580.0 5.5 copy-start.4
  (7 other events, 7.7 us)
Sparse Core Ops, SparseCore 0:
  9.9 37.0 all-gather.8
  48.9 34.3 all-gather.4
  85.2 34.3 all-gather.6
  126.1 56.5 all-gather.10
  453.7 125.2 all-reduce.1
